TPU v7x, 128 devices: a whole 4x4x4 slice. The times are simulated.
128 devices in a mesh: group: 8 (over x, core), ctx: 16 (over y, z).
Axes of the slice: x: 4, y: 4, z: 4, core: 2. Of those that a mesh axis runs over, the one named last changes fastest.
Arguments:
- query_rows: bfloat16 [8, 4096, 4096], P('group', 'ctx'), may hold values from -250 to 250
- key_rows: bfloat16 [8, 4096, 512], P('group', 'ctx'), may hold values from -7 to 7
- value_rows: bfloat16 [8, 4096, 512], P('group', 'ctx'), may hold values from -6 to 6
- documents: int32 [8, 4096], P('group', 'ctx'), may hold values from 0 to 3, never falling along the last dimension, each value on 1 to 2560 neighbouring positions
- owners: int32 [8, 128, 1], P('group', 'ctx'), may hold values from 0 to 7; in each aligned block of 8 rows (0 to 7, 8 to 15, ..., all dimensions but the last counted through in order) at most 2 rows name the same one
Outputs:
- attended: bfloat16 [8, 4096, 4096], P('group', 'ctx')
- page_pool: bfloat16 [8, 256, 2, 128, 128], P('group', 'ctx')
- page_scales: bfloat16 [8, 256, 2], P('group', 'ctx')
Inputs may be any that keep to these rules, and one draw needn't show every extreme that they name: `documents`: document numbers never fall along a group's tokens; each document has at most 2560 tokens. `owners`: among the pages of one device, no owner is named more than 2 times.
All inputs are finite; a program needn't handle non-finite values.
Results may differ from a plain program's by a relative error of at most 0.0028.
Values may be sent and summed in bfloat16 or wider, within the bound.
No kernel may reach another device: no remote copies, remote signals or barrier semaphores. Data moves between devices by JAX's collectives and lax.ppermute only.
A program may use at most 128 MiB of HBM per device.

v0:
```python
import math

import jax
import jax.numpy as jnp
from jax import lax
from jax.experimental import pallas as pl
from jax.experimental.pallas import tpu as pltpu
from jax.sharding import PartitionSpec as P


E = 128
HQ = 32
HK = 4
PAGE = 128
T = 256
REP = HQ // HK
SIDE = 4
ROWS = T + 8
W = 2 * HK * E
epsilon = 1e-06
exp2_scale = math.log2(math.e) / math.sqrt(E)
low = -1e30


def toward(leading, step):
    pairs = []
    for group in range(8):
        for y in range(SIDE):
            for z in range(SIDE):
                if (group % 2 == 0) == leading:
                    to = SIDE * y + (z + step) % SIDE
                else:
                    to = SIDE * ((y + step) % SIDE) + z
                pairs.append((SIDE * SIDE * group + SIDE * y + z, SIDE * SIDE * group + to))
    return pairs


def attend_stage(places, pieces, first, last):
    count = len(places)

    def kernel(*refs):
        refs = list(refs)
        here_ref, doc_ref, start_ref, q_ref = refs[:4]
        del refs[:4]
        if not first:
            acc_in, m_in, l_in = refs[:3]
            del refs[:3]
        operands = refs[: len(pieces)]
        del refs[: len(pieces)]
        if last:
            out_ref = refs.pop(0)
        else:
            acc_out, m_out, l_out = refs[:3]
            del refs[:3]
        kv = refs[0]
        s_ref = refs[1:3]
        m_ref = refs[3:5]
        acc, l_ref, lists, sems = refs[5:]
        step = pl.program_id(0)
        starts = start_ref[0:1, :]
        in_first_doc = starts == 0
        lane = lax.broadcasted_iota(jnp.int32, (T, T), 1)
        row = lax.broadcasted_iota(jnp.int32, (T, T), 0)

        def load():
            copies = []
            at = 0
            for k, (ref, n) in enumerate(zip(operands, pieces)):
                copy = pltpu.make_async_copy(ref, kv.at[pl.ds(at, n)], sems.at[k])
                copy.start()
                copies.append(copy)
                at += n
            for copy in copies:
                copy.wait()
            own = here_ref[0]
            swapped = here_ref[1] == 1
            doc = doc_ref[0].astype(jnp.float32)
            y, z = lax.shift_right_logical(own, 2), own & 3
            n = jnp.int32(0)
            has = jnp.int32(0)
            edge = jnp.int32(0)
            edge_row = jnp.int32(0)
            for slot in range(1 if first else 0, count):
                ids = kv[slot, T : T + 8, 0:T].astype(jnp.float32)[0:1]
                same = jnp.sum(jnp.where(ids == doc, 1.0, 0.0)).astype(jnp.int32)
                lead, follow = places[slot]
                dy = jnp.where(swapped, lead, follow)
                dz = jnp.where(swapped, follow, lead)
                chunk = ((y + dy) & 3) * SIDE + ((z + dz) & 3)
                same = jnp.where(chunk < own, same, 0)
                lists[n] = slot
                n = n + jnp.where(same == T, 1, 0)
                part = (same > 0) & (same < T)
                has = jnp.where(part, 1, has)
                edge = jnp.where(part, slot, edge)
                edge_row = jnp.where(part, T - same, edge_row)
            lists[16] = n
            lists[17] = has
            lists[18] = edge
            lists[19] = edge_row

        def scores(g, slot, h):
            keys = kv[slot, 0:T, pl.ds(pl.multiple_of(g * E, E), E)]
            queries = q_ref[:, pl.ds(h * E, E)]
            return lax.dot_general(
                keys, queries, (((1,), (1,)), ((), ())), preferred_element_type=jnp.float32
            )

        def top(s):
            return jnp.max(s.reshape(T // 8, 8, T), axis=0)

        def keep(b, h, place, s):
            s_ref[b][h, pl.ds(place * T, T), :] = s
            m_ref[b][h] = jnp.maximum(m_ref[b][h], top(s))

        def weigh(g, b, h, sources, largest):
            total, sums = None, None
            for place, slot in sources:
                p = jnp.exp2((s_ref[b][h, pl.ds(place * T, T), :] - largest[h]) * exp2_scale)
                part = jnp.sum(p.reshape(T // 8, 8, T), axis=0)
                at = pl.multiple_of(lax.shift_right_logical(g, 1) * E, E)
                values = kv[slot, pl.ds(at, E), pl.ds(pl.multiple_of(HK * E + (g & 1) * T, T), T)]
                product = lax.dot_general(
                    values, p.astype(jnp.bfloat16), (((1,), (0,)), ((), ())),
                    preferred_element_type=jnp.float32,
                )
                total = product if total is None else total + product
                sums = part if sums is None else sums + part
            l_ref[h] += sums
            acc[h] += total

        def turn(scoring, weighing, b):
            score_g, weigh_g, a = step, step - 1, 1 - b
            n, has, edge, edge_row = lists[16], lists[17], lists[18], lists[19]
            if weighing:
                largest = []
                for h in range(REP):
                    m = jnp.max(m_ref[a][h], axis=0, keepdims=True)
                    if first:
                        acc[h] = jnp.zeros((E, T), jnp.float32)
                        l_ref[h] = jnp.zeros((8, T), jnp.float32)
                    else:
                        before = m_in[h, 0:1]
                        m = jnp.maximum(before, jnp.where(in_first_doc, m, low))
                        shrink = jnp.exp2((before - m) * exp2_scale)
                        acc[h] = acc_in[h] * shrink
                        l_ref[h] = l_in[h] * shrink
                    if not last:
                        m_out[h] = jnp.broadcast_to(m, (8, T))
                    largest.append(m)
                prior = [jnp.where(in_first_doc, m, -low) for m in largest]
            if scoring:
                m_ref[b][...] = jnp.full((REP, 8, T), low, jnp.float32)

            def whole(at, width):
                for h in range(REP):
                    if scoring:
                        for w in range(width):
                            keep(b, h, 2 + at + w, scores(score_g, lists[at + w], h))
                    if weighing:
                        sources = [(2 + at + w, lists[at + w]) for w in range(width)]
                        weigh(weigh_g, a, h, sources, prior)

            def pair(i, _):
                whole(2 * i, 2)
                return 0

            def single(i, _):
                whole(i, 1)
                return 0

            def cut(i, _):
                for h in range(REP):
                    if scoring:
                        s = scores(score_g, edge, h)
                        keep(b, h, 1, jnp.where(row >= edge_row, s, low))
                    if weighing:
                        weigh(weigh_g, a, h, [(1, edge)], prior)
                return 0

            pairs = lax.shift_right_logical(n, 1)
            lax.fori_loop(0, pairs, pair, 0)
            lax.fori_loop(2 * pairs, n, single, 0)
            lax.fori_loop(0, has, cut, 0)
            for h in range(REP):
                if first:
                    if scoring:
                        s = scores(score_g, 0, h)
                        s = jnp.where((row >= starts) & (row <= lane), s, low)
                        m_ref[b][h] = jnp.where(in_first_doc, m_ref[b][h], low)
                        keep(b, h, 0, s)
                    if weighing:
                        weigh(weigh_g, a, h, [(0, 0)], largest)
                if weighing:
                    if last:
                        total = jnp.sum(l_ref[h], axis=0, keepdims=True)
                        result = (acc[h] / total).astype(jnp.bfloat16)
                        out_ref[:, pl.ds(h * E, E)] = result.T
                    else:
                        acc_out[h] = acc[h]
                        l_out[h] = l_ref[h]

        @pl.when(step == 0)
        def _():
            load()
            turn(True, False, 0)

        @pl.when((step == 1) | (step == 3))
        def _():
            turn(True, True, 1)

        @pl.when(step == 2)
        def _():
            turn(True, True, 0)

        @pl.when(step == HK)
        def _():
            turn(False, True, 0)

    def now(i):
        return jnp.minimum(i, HK - 1)

    def behind(i):
        return jnp.maximum(i - 1, 0)

    carry_specs = [
        pl.BlockSpec((REP, E, T), lambda i: (behind(i), 0, 0)),
        pl.BlockSpec((REP, 8, T), lambda i: (behind(i), 0, 0)),
        pl.BlockSpec((REP, 8, T), lambda i: (behind(i), 0, 0)),
    ]
    carry_shapes = [
        jax.ShapeDtypeStruct((HQ, E, T), jnp.float32),
        jax.ShapeDtypeStruct((HQ, 8, T), jnp.float32),
        jax.ShapeDtypeStruct((HQ, 8, T), jnp.float32),
    ]
    in_specs = [
        pl.BlockSpec(memory_space=pltpu.SMEM),
        pl.BlockSpec(memory_space=pltpu.SMEM),
        pl.BlockSpec((8, T), lambda i: (0, 0)),
        pl.BlockSpec((T, REP * E), lambda i: (0, now(i))),
    ]
    if not first:
        in_specs += carry_specs
    in_specs += [pl.BlockSpec(memory_space=pl.ANY)] * len(pieces)
    if last:
        out_specs = pl.BlockSpec((T, REP * E), lambda i: (0, behind(i)))
        out_shape = jax.ShapeDtypeStruct((T, HQ * E), jnp.bfloat16)
    else:
        out_specs, out_shape = carry_specs, carry_shapes
    return pl.pallas_call(
        kernel,
        grid=(HK + 1,),
        in_specs=in_specs,
        out_specs=out_specs,
        out_shape=out_shape,
        scratch_shapes=[
            pltpu.VMEM((count, ROWS, W), jnp.bfloat16),
            pltpu.VMEM((REP, (count + 2) * T, T), jnp.float32),
            pltpu.VMEM((REP, (count + 2) * T, T), jnp.float32),
            pltpu.VMEM((REP, 8, T), jnp.float32),
            pltpu.VMEM((REP, 8, T), jnp.float32),
            pltpu.VMEM((REP, E, T), jnp.float32),
            pltpu.VMEM((REP, 8, T), jnp.float32),
            pltpu.SMEM((32,), jnp.int32),
            pltpu.SemaphoreType.DMA((len(pieces),)),
        ],
        compiler_params=pltpu.CompilerParams(
            dimension_semantics=("arbitrary",), vmem_limit_bytes=58 * 1024 * 1024
        ),
        cost_estimate=pl.CostEstimate(
            flops=count * T * T * E * HQ * 4, transcendentals=0, bytes_accessed=1 << 22
        ),
        name="attend_first" if first else "attend_last" if last else "attend_middle",
    )


def pack_pages(keys, values, owner_list):
    def kernel(owner_ref, k_ref, v_ref, out_ref):
        out_ref[...] = jnp.zeros(out_ref.shape, out_ref.dtype)
        lane = lax.broadcasted_iota(jnp.int32, (8, E), 1)
        for page in range(8):
            block, head = page // HK, page % HK
            owner = owner_ref[page]
            rank = jnp.int32(0)
            for other in range(page):
                rank = rank + jnp.where(owner_ref[other] == owner, 1, 0)
            slot = owner * 2 + jnp.minimum(rank, 1)
            scales = []
            for which, ref in enumerate((k_ref, v_ref)):
                x = ref[block * PAGE : (block + 1) * PAGE, head * E : (head + 1) * E]
                x = x.astype(jnp.float32)
                size = jnp.max(jnp.max(jnp.abs(x), axis=0, keepdims=True), axis=1, keepdims=True)
                scale = (size + epsilon).astype(jnp.bfloat16).astype(jnp.float32)
                out_ref[slot, which * PAGE : (which + 1) * PAGE, :] = (x / scale).astype(
                    jnp.bfloat16
                )
                scales.append(scale)
            both = jnp.where(lane == 0, scales[0], jnp.where(lane == 1, scales[1], 0.0))
            out_ref[slot, 2 * PAGE : 2 * PAGE + 8, :] = both.astype(jnp.bfloat16)

    return pl.pallas_call(
        kernel,
        in_specs=[
            pl.BlockSpec(memory_space=pltpu.SMEM),
            pl.BlockSpec(memory_space=pltpu.VMEM),
            pl.BlockSpec(memory_space=pltpu.VMEM),
        ],
        out_specs=pl.BlockSpec(memory_space=pltpu.VMEM),
        out_shape=jax.ShapeDtypeStruct((16, 2 * PAGE + 8, E), jnp.bfloat16),
        name="pack_pages",
    )(owner_list, keys, values)


def prepare(keys, values, docs):
    def kernel(k_ref, v_ref, doc_ref, chunk_ref, start_ref):
        docs = doc_ref[...]
        chunk_ref[0:T, 0 : HK * E] = k_ref[...]
        for g in range(HK):
            at, lane = g // 2 * E, HK * E + g % 2 * T
            chunk_ref[at : at + E, lane : lane + T] = v_ref[:, g * E : (g + 1) * E].T
        chunk_ref[T:ROWS, 0:T] = jnp.broadcast_to(docs.astype(jnp.float32), (8, T)).astype(
            jnp.bfloat16
        )
        chunk_ref[T:ROWS, T:W] = jnp.zeros((8, W - T), jnp.bfloat16)
        starts = jnp.zeros((1, T), jnp.int32)
        for doc in range(1, 4):
            before = jnp.sum(
                jnp.where(docs < doc, 1.0, 0.0), axis=1, keepdims=True
            ).astype(jnp.int32)
            starts = jnp.where(docs == doc, before, starts)
        start_ref[...] = jnp.broadcast_to(starts, (8, T))

    vmem = pl.BlockSpec(memory_space=pltpu.VMEM)
    return pl.pallas_call(
        kernel,
        in_specs=[vmem] * 3,
        out_specs=[vmem] * 2,
        out_shape=[
            jax.ShapeDtypeStruct((ROWS, W), jnp.bfloat16),
            jax.ShapeDtypeStruct((8, T), jnp.int32),
        ],
        name="prepare",
    )(keys, values, docs)


def whole_step(query_rows, key_rows, value_rows, documents, owners):
    queries, keys, values = query_rows[0], key_rows[0], value_rows[0]
    docs = documents[0]
    here = jnp.stack([lax.axis_index("ctx"), lax.axis_index("group") & 1]).astype(jnp.int32)

    def send(x, leading, step):
        return lax.ppermute(x, ("group", "ctx"), toward(leading, step))

    def chunks(x):
        return x.reshape(-1, ROWS, W)

    own, starts = prepare(keys, values, documents)
    up, down = send(own, True, 1), send(own, True, -1)
    far = send(own, True, 2)
    own_up, own_down = send(own, False, 1), send(own, False, -1)
    packed = pack_pages(keys, values, owners[0, :, 0])
    arrived = lax.all_to_all(
        packed.reshape(8, 2, 2 * PAGE + 8, E), "group", split_axis=0, concat_axis=0, tiled=True
    ).reshape(16, 2 * PAGE + 8, E)
    up, down, packed = lax.optimization_barrier((up, down, packed))
    up_up, up_down = send(up, False, 1), send(up, False, -1)
    two = jnp.concatenate([down, far])
    two_down, two_up = send(two, False, -1), send(two, False, 1)
    own_far = send(own_up, False, 1)
    up_far = send(up_up, False, 1)
    two_far = send(two_down, False, -1)

    steps = (0, -1, 1, 2)
    common = (here, docs, starts, queries)

    def stage(follows, first, last, carry, operands):
        places = [(d, s) for s in follows for d in steps]
        pieces = (1, 1, 2) * len(follows)
        return attend_stage(places, pieces, first, last)(*common, *carry, *map(chunks, operands))

    carry = stage((0,), True, False, (), (own, up, two))
    carry = stage(
        (-1, 1), False, False, carry, (own_up, up_up, two_up, own_down, up_down, two_down)
    )
    attended = stage((2,), False, True, carry, (own_far, up_far, two_far))

    pool = arrived[:, : 2 * PAGE].reshape(1, 16, 2, PAGE, E)
    return attended[None], pool, arrived[None, :, 2 * PAGE, :2]


def solution(mesh):
    placed = (
        P("group", "ctx", None),
        P("group", "ctx", None),
        P("group", "ctx", None),
        P("group", "ctx"),
        P("group", "ctx", None),
    )
    return jax.shard_map(
        whole_step,
        mesh=mesh,
        in_specs=placed,
        out_specs=(
            P("group", "ctx", None),
            P("group", "ctx", None, None, None),
            P("group", "ctx", None),
        ),
        check_vma=False,
    )
```

profile of v0, /device:TPU:28, one launch (start us, length us, event | category | flops | bytes accessed | tf_op | source)
XLA Modules:
  0.0 94.0 jit_solution(16644985265396062853)
XLA Ops:
  0.6 2.0 %prepare.1 = (bf16[264,1024]{1,0:T(8,128)(2,1)}, s32[8,256]{1,0:T(8,128)}) custom-call(bf16[256,512]{1,0:T(8,128)(2,1)} %bitcast.27, bf16[256,512]{1,0:T(8,128)(2,1)} %bitcast.29, s32[1,256]{1,0:T(1,128)} %doc_ref.1), custom_call_target="tpu_custom_call" | custom-call | tf_op jit(solution)/shard_map/prepare/pallas_call | solution.py:334
  2.6 1.9 %collective-permute-start = (bf16[264,1024]{1,0:T(8,128)(2,1)}, bf16[264,1024]{1,0:T(8,128)(2,1)S(1)}, u32[]{:S(2)}, u32[]{:S(2)}) collective-permute-start(bf16[264,1024]{1,0:T(8,128)(2,1)} %get-tuple-element.14), channel_id=1, source_target_pairs={{0,1},{1,2},{2,3},{3,0},{4,5},{5,6},{6,7},{7,4},{8,9},{9,10},{10,1... | collective-permute-start | bytes 1622024 | tf_op jit(solution)/shard_map/ppermute | solution.py:352
  4.5 2.1 %collective-permute-start.1 = (bf16[264,1024]{1,0:T(8,128)(2,1)}, bf16[264,1024]{1,0:T(8,128)(2,1)S(1)}, u32[]{:S(2)}, u32[]{:S(2)}) collective-permute-start(bf16[264,1024]{1,0:T(8,128)(2,1)} %get-tuple-element.14), channel_id=1, source_target_pairs={{0,3},{1,0},{2,1},{3,2},{4,7},{5,4},{6,5},{7,6},{8,11},{9,8},{10,9... | collective-permute-start | bytes 1622024 | tf_op jit(solution)/shard_map/ppermute | solution.py:352
  6.7 1.9 %collective-permute-start.2 = (bf16[264,1024]{1,0:T(8,128)(2,1)}, bf16[264,1024]{1,0:T(8,128)(2,1)S(1)}, u32[]{:S(2)}, u32[]{:S(2)}) collective-permute-start(bf16[264,1024]{1,0:T(8,128)(2,1)} %get-tuple-element.14), channel_id=1, source_target_pairs={{0,2},{1,3},{2,0},{3,1},{4,6},{5,7},{6,4},{7,5},{8,10},{9,11},{10,... | collective-permute-start | bytes 1622024 | tf_op jit(solution)/shard_map/ppermute | solution.py:352
  8.5 2.3 %pack_pages.1 = bf16[16,264,128]{2,1,0:T(8,128)(2,1)} custom-call(s32[8]{0:T(128)} %bitcast.35, bf16[256,512]{1,0:T(8,128)(2,1)} %bitcast.28, bf16[256,512]{1,0:T(8,128)(2,1)} %bitcast.30), custom_call_target="tpu_custom_call" | custom-call | tf_op jit(solution)/shard_map/pack_pages/pallas_call | solution.py:301
  10.9 3.3 %collective-permute-done = bf16[264,1024]{1,0:T(8,128)(2,1)S(1)} collective-permute-done((bf16[264,1024]{1,0:T(8,128)(2,1)}, bf16[264,1024]{1,0:T(8,128)(2,1)S(1)}, u32[]{:S(2)}, u32[]{:S(2)}) %collective-permute-start) | collective-permute-done | bytes 540704 | tf_op jit(solution)/shard_map/ppermute | solution.py:352
  14.2 0.0 copy-start.2
  14.2 0.8 copy-done.2
  15.0 4.7 %collective-permute-done.1 = bf16[264,1024]{1,0:T(8,128)(2,1)S(1)} collective-permute-done((bf16[264,1024]{1,0:T(8,128)(2,1)}, bf16[264,1024]{1,0:T(8,128)(2,1)S(1)}, u32[]{:S(2)}, u32[]{:S(2)}) %collective-permute-start.1) | collective-permute-done | bytes 540704 | tf_op jit(solution)/shard_map/ppermute | solution.py:352
  19.7 1.7 %collective-permute-done.2 = bf16[264,1024]{1,0:T(8,128)(2,1)S(1)} collective-permute-done((bf16[264,1024]{1,0:T(8,128)(2,1)}, bf16[264,1024]{1,0:T(8,128)(2,1)S(1)}, u32[]{:S(2)}, u32[]{:S(2)}) %collective-permute-start.2) | collective-permute-done | bytes 540704 | tf_op jit(solution)/shard_map/ppermute | solution.py:352
  21.5 0.0 copy-start
  21.5 0.8 collective-permute-start.8
  22.3 2.5 %collective-permute-start.3 = (bf16[264,1024]{1,0:T(8,128)(2,1)}, bf16[264,1024]{1,0:T(8,128)(2,1)}, u32[]{:S(2)}, u32[]{:S(2)}) collective-permute-start(bf16[264,1024]{1,0:T(8,128)(2,1)} %get-tuple-element.14), channel_id=1, source_target_pairs={{0,4},{1,5},{2,6},{3,7},{4,8},{5,9},{6,10},{7,11},{8,12},{9,13},{1... | collective-permute-start | bytes 1622024 | tf_op jit(solution)/shard_map/ppermute | solution.py:352
  24.8 0.0 collective-permute-start.5
  24.8 0.0 copy-done
  24.8 4.8 %all-to-all-start = ((bf16[8,2,264,128]{3,2,1,0:T(8,128)(2,1)}), bf16[8,2,264,128]{3,2,1,0:T(8,128)(2,1)S(1)}, u32[]{:S(2)}, u32[]{:S(2)}) async-start(bf16[8,2,264,128]{3,2,1,0:T(8,128)(2,1)} %bitcast.20), calls=%async_computation | async-start | bytes 2162688 | tf_op jit(solution)/shard_map/all_to_all | solution.py:362
  29.6 2.0 %collective-permute-start.6 = (bf16[264,1024]{1,0:T(8,128)(2,1)}, bf16[264,1024]{1,0:T(8,128)(2,1)}, u32[]{:S(2)}, u32[]{:S(2)}) collective-permute-start(bf16[264,1024]{1,0:T(8,128)(2,1)} %get-tuple-element.14), channel_id=1, source_target_pairs={{0,12},{1,13},{2,14},{3,15},{4,0},{5,1},{6,2},{7,3},{8,4},{9,5},{1... | collective-permute-start | bytes 1622024 | tf_op jit(solution)/shard_map/ppermute | solution.py:352
  31.6 1.2 %collective-permute-start.4 = (bf16[264,1024]{1,0:T(8,128)(2,1)}, bf16[264,1024]{1,0:T(8,128)(2,1)}, u32[]{:S(2)}, u32[]{:S(2)}) collective-permute-start(bf16[264,1024]{1,0:T(8,128)(2,1)} %copy-done.2), channel_id=1, source_target_pairs={{0,4},{1,5},{2,6},{3,7},{4,8},{5,9},{6,10},{7,11},{8,12},{9,13},{1... | collective-permute-start | bytes 1622024 | tf_op jit(solution)/shard_map/ppermute | solution.py:352
  32.9 0.0 collective-permute-done.3
  32.9 0.8 collective-permute-start.7
  33.7 0.7 pad_add_fusion.refs_0_
  34.3 3.6 %collective-permute-done.8 = bf16[528,1024]{1,0:T(8,128)(2,1)S(1)} collective-permute-done((bf16[528,1024]{1,0:T(8,128)(2,1)S(1)}, bf16[528,1024]{1,0:T(8,128)(2,1)S(1)}, u32[]{:S(2)}, u32[]{:S(2)}) %collective-permute-start.8) | collective-permute-done | bytes 1081376 | tf_op jit(solution)/shard_map/ppermute | solution.py:352
  37.9 0.0 copy-start.1
  37.9 0.0 collective-permute-start.11
  37.9 8.8 %attend_first.1 = (f32[32,128,256]{2,1,0:T(8,128)}, f32[32,8,256]{2,1,0:T(8,128)}, f32[32,8,256]{2,1,0:T(8,128)}) custom-call(s32[2]{0:T(128)} %pad_add_fusion.refs_0_, s32[256]{0:T(256)} %bitcast.32, s32[8,256]{1,0:T(8,128)} %get-tuple-element.13.refs_2_, bf16[256,4096]{1,0:T(8,128)(2,1)} %bitcast.37, bf16[1,264,1024]{2,1,0:T(8,128)(2,1)} %bitcast.6.refs_4_, ...), custom_call_target="tpu_custom_call" | custom-call | flops 4294967296 | bytes 4194304 | tf_op jit(solution)/shard_map/attend_first/pallas_call | solution.py:379
  46.8 0.0 copy-done.1
  46.8 0.0 all-to-all-done
  46.8 1.1 %slice.8 = bf16[16,256,128]{2,1,0:T(8,128)(2,1)} slice(bf16[16,264,128]{2,1,0:T(8,128)(2,1)S(1)} %bitcast.24), slice={[0:16], [0:256], [0:128]} | slice | bytes 2097152 | tf_op jit(solution)/shard_map/slice | solution.py:387
  47.9 0.6 copy.10
  48.5 0.0 collective-permute-done.6
  48.5 2.8 %collective-permute-start.9 = (bf16[264,1024]{1,0:T(8,128)(2,1)}, bf16[264,1024]{1,0:T(8,128)(2,1)S(1)}, u32[]{:S(2)}, u32[]{:S(2)}) collective-permute-start(bf16[264,1024]{1,0:T(8,128)(2,1)} %collective-permute-done.3), channel_id=1, source_target_pairs={{0,4},{1,5},{2,6},{3,7},{4,8},{5,9},{6,10},{7,11},{8,12},{9,13},{1... | collective-permute-start | bytes 1622024 | tf_op jit(solution)/shard_map/ppermute | solution.py:352
  51.3 0.0 collective-permute-done.4
  51.3 1.7 %collective-permute-start.10 = (bf16[264,1024]{1,0:T(8,128)(2,1)}, bf16[264,1024]{1,0:T(8,128)(2,1)S(1)}, u32[]{:S(2)}, u32[]{:S(2)}) collective-permute-start(bf16[264,1024]{1,0:T(8,128)(2,1)} %collective-permute-done.4), channel_id=1, source_target_pairs={{0,4},{1,5},{2,6},{3,7},{4,8},{5,9},{6,10},{7,11},{8,12},{9,13},{1... | collective-permute-start | bytes 1622024 | tf_op jit(solution)/shard_map/ppermute | solution.py:352
  53.1 0.0 collective-permute-done.7
  53.1 0.0 collective-permute-done.5
  53.1 23.0 %attend_middle.1 = (f32[32,128,256]{2,1,0:T(8,128)}, f32[32,8,256]{2,1,0:T(8,128)}, f32[32,8,256]{2,1,0:T(8,128)}) custom-call(s32[2]{0:T(128)} %pad_add_fusion.refs_0_, s32[256]{0:T(256)} %bitcast.33, s32[8,256]{1,0:T(8,128)} %get-tuple-element.13.refs_2_, bf16[256,4096]{1,0:T(8,128)(2,1)} %bitcast.38, f32[32,128,256]{2,1,0:T(8,128)} %get-tuple-element.17.refs_4_, ...), custom_call_target="tpu_custom_call" | custom-call | flops 8589934592 | bytes 4194304 | tf_op jit(solution)/shard_map/attend_middle/pallas_call | solution.py:379
  76.1 0.0 collective-permute-done.9
  76.1 0.0 copy-start.3
  76.1 0.0 collective-permute-done.10
  76.1 0.0 copy-start.4
  76.2 0.0 collective-permute-done.11
  76.2 0.8 copy-done.3
  76.9 0.2 copy-done.4
  77.1 16.7 %attend_last.1 = bf16[256,4096]{1,0:T(8,128)(2,1)} custom-call(s32[2]{0:T(128)} %pad_add_fusion.refs_0_, s32[256]{0:T(256)} %bitcast.34, s32[8,256]{1,0:T(8,128)} %get-tuple-element.13.refs_2_, bf16[256,4096]{1,0:T(8,128)(2,1)} %bitcast.39, f32[32,128,256]{2,1,0:T(8,128)} %get-tuple-element.20.refs_4_, f32[32,8,256]{2,1,0:T(8,128)} %get-tuple-element.21.refs_5_, ...), custom_call_target="tpu_custom_call" | custom-call | flops 4294967296 | bytes 4194304 | tf_op jit(solution)/shard_map/attend_last/pallas_call | solution.py:379
  (3 shorter events, 0.1 us)
Async XLA Ops:
  2.6 11.6 %collective-permute-start = (bf16[264,1024]{1,0:T(8,128)(2,1)}, bf16[264,1024]{1,0:T(8,128)(2,1)S(1)}, u32[]{:S(2)}, u32[]{:S(2)}) collective-permute-start(bf16[264,1024]{1,0:T(8,128)(2,1)} %get-tuple-element.14), channel_id=1, source_target_pairs={{0,1},{1,2},{2,3},{3,0},{4,5},{5,6},{6,7},{7,4},{8,9},{9,10},{10,1... | collective-permute-start | bytes 1622024 | tf_op jit(solution)/shard_map/ppermute | solution.py:352
  4.5 15.1 %collective-permute-start.1 = (bf16[264,1024]{1,0:T(8,128)(2,1)}, bf16[264,1024]{1,0:T(8,128)(2,1)S(1)}, u32[]{:S(2)}, u32[]{:S(2)}) collective-permute-start(bf16[264,1024]{1,0:T(8,128)(2,1)} %get-tuple-element.14), channel_id=1, source_target_pairs={{0,3},{1,0},{2,1},{3,2},{4,7},{5,4},{6,5},{7,6},{8,11},{9,8},{10,9... | collective-permute-start | bytes 1622024 | tf_op jit(solution)/shard_map/ppermute | solution.py:352
  6.7 14.8 %collective-permute-start.2 = (bf16[264,1024]{1,0:T(8,128)(2,1)}, bf16[264,1024]{1,0:T(8,128)(2,1)S(1)}, u32[]{:S(2)}, u32[]{:S(2)}) collective-permute-start(bf16[264,1024]{1,0:T(8,128)(2,1)} %get-tuple-element.14), channel_id=1, source_target_pairs={{0,2},{1,3},{2,0},{3,1},{4,6},{5,7},{6,4},{7,5},{8,10},{9,11},{10,... | collective-permute-start | bytes 1622024 | tf_op jit(solution)/shard_map/ppermute | solution.py:352
  14.2 0.8 copy-start.2
  21.5 3.3 %copy-start = (bf16[528,1024]{1,0:T(8,128)(2,1)}, bf16[528,1024]{1,0:T(8,128)(2,1)S(1)}, u32[]{:S(2)}) copy-start(bf16[528,1024]{1,0:T(8,128)(2,1)S(1)} %constant_dynamic-update-slice_fusion) | copy-start | bytes 3244036
  21.5 16.4 %collective-permute-start.8 = (bf16[528,1024]{1,0:T(8,128)(2,1)S(1)}, bf16[528,1024]{1,0:T(8,128)(2,1)S(1)}, u32[]{:S(2)}, u32[]{:S(2)}) collective-permute-start(bf16[528,1024]{1,0:T(8,128)(2,1)S(1)} %constant_dynamic-update-slice_fusion), channel_id=1, source_target_pairs={{0,12},{1,13},{2,14},{3,15},{4,0},{5,1},{6,2},{7,3},{8,4},{9,5},{1... | collective-permute-start | bytes 3244040 | tf_op jit(solution)/shard_map/ppermute | solution.py:352
  22.3 10.6 %collective-permute-start.3 = (bf16[264,1024]{1,0:T(8,128)(2,1)}, bf16[264,1024]{1,0:T(8,128)(2,1)}, u32[]{:S(2)}, u32[]{:S(2)}) collective-permute-start(bf16[264,1024]{1,0:T(8,128)(2,1)} %get-tuple-element.14), channel_id=1, source_target_pairs={{0,4},{1,5},{2,6},{3,7},{4,8},{5,9},{6,10},{7,11},{8,12},{9,13},{1... | collective-permute-start | bytes 1622024 | tf_op jit(solution)/shard_map/ppermute | solution.py:352
  24.8 28.3 %collective-permute-start.5 = (bf16[528,1024]{1,0:T(8,128)(2,1)S(1)}, bf16[528,1024]{1,0:T(8,128)(2,1)}, u32[]{:S(2)}, u32[]{:S(2)}) collective-permute-start(bf16[528,1024]{1,0:T(8,128)(2,1)S(1)} %constant_dynamic-update-slice_fusion), channel_id=1, source_target_pairs={{0,4},{1,5},{2,6},{3,7},{4,8},{5,9},{6,10},{7,11},{8,12},{9,13},{1... | collective-permute-start | bytes 3244040 | tf_op jit(solution)/shard_map/ppermute | solution.py:352
  24.8 22.0 %all-to-all-start = ((bf16[8,2,264,128]{3,2,1,0:T(8,128)(2,1)}), bf16[8,2,264,128]{3,2,1,0:T(8,128)(2,1)S(1)}, u32[]{:S(2)}, u32[]{:S(2)}) async-start(bf16[8,2,264,128]{3,2,1,0:T(8,128)(2,1)} %bitcast.20), calls=%async_computation | async-start | bytes 2162688 | tf_op jit(solution)/shard_map/all_to_all | solution.py:362
  29.6 18.9 %collective-permute-start.6 = (bf16[264,1024]{1,0:T(8,128)(2,1)}, bf16[264,1024]{1,0:T(8,128)(2,1)}, u32[]{:S(2)}, u32[]{:S(2)}) collective-permute-start(bf16[264,1024]{1,0:T(8,128)(2,1)} %get-tuple-element.14), channel_id=1, source_target_pairs={{0,12},{1,13},{2,14},{3,15},{4,0},{5,1},{6,2},{7,3},{8,4},{9,5},{1... | collective-permute-start | bytes 1622024 | tf_op jit(solution)/shard_map/ppermute | solution.py:352
  31.6 19.7 %collective-permute-start.4 = (bf16[264,1024]{1,0:T(8,128)(2,1)}, bf16[264,1024]{1,0:T(8,128)(2,1)}, u32[]{:S(2)}, u32[]{:S(2)}) collective-permute-start(bf16[264,1024]{1,0:T(8,128)(2,1)} %copy-done.2), channel_id=1, source_target_pairs={{0,4},{1,5},{2,6},{3,7},{4,8},{5,9},{6,10},{7,11},{8,12},{9,13},{1... | collective-permute-start | bytes 1622024 | tf_op jit(solution)/shard_map/ppermute | solution.py:352
  32.9 20.2 %collective-permute-start.7 = (bf16[264,1024]{1,0:T(8,128)(2,1)}, bf16[264,1024]{1,0:T(8,128)(2,1)}, u32[]{:S(2)}, u32[]{:S(2)}) collective-permute-start(bf16[264,1024]{1,0:T(8,128)(2,1)} %copy-done.2), channel_id=1, source_target_pairs={{0,12},{1,13},{2,14},{3,15},{4,0},{5,1},{6,2},{7,3},{8,4},{9,5},{1... | collective-permute-start | bytes 1622024 | tf_op jit(solution)/shard_map/ppermute | solution.py:352
  37.9 8.9 %copy-start.1 = (bf16[528,1024]{1,0:T(8,128)(2,1)}, bf16[528,1024]{1,0:T(8,128)(2,1)S(1)}, u32[]{:S(2)}) copy-start(bf16[528,1024]{1,0:T(8,128)(2,1)S(1)} %collective-permute-done.8) | copy-start | bytes 3244036
  37.9 38.2 %collective-permute-start.11 = (bf16[528,1024]{1,0:T(8,128)(2,1)S(1)}, bf16[528,1024]{1,0:T(8,128)(2,1)}, u32[]{:S(2)}, u32[]{:S(2)}) collective-permute-start(bf16[528,1024]{1,0:T(8,128)(2,1)S(1)} %collective-permute-done.8), channel_id=1, source_target_pairs={{0,12},{1,13},{2,14},{3,15},{4,0},{5,1},{6,2},{7,3},{8,4},{9,5},{1... | collective-permute-start | bytes 3244040 | tf_op jit(solution)/shard_map/ppermute | solution.py:352
  48.5 27.6 %collective-permute-start.9 = (bf16[264,1024]{1,0:T(8,128)(2,1)}, bf16[264,1024]{1,0:T(8,128)(2,1)S(1)}, u32[]{:S(2)}, u32[]{:S(2)}) collective-permute-start(bf16[264,1024]{1,0:T(8,128)(2,1)} %collective-permute-done.3), channel_id=1, source_target_pairs={{0,4},{1,5},{2,6},{3,7},{4,8},{5,9},{6,10},{7,11},{8,12},{9,13},{1... | collective-permute-start | bytes 1622024 | tf_op jit(solution)/shard_map/ppermute | solution.py:352
  51.3 24.8 %collective-permute-start.10 = (bf16[264,1024]{1,0:T(8,128)(2,1)}, bf16[264,1024]{1,0:T(8,128)(2,1)S(1)}, u32[]{:S(2)}, u32[]{:S(2)}) collective-permute-start(bf16[264,1024]{1,0:T(8,128)(2,1)} %collective-permute-done.4), channel_id=1, source_target_pairs={{0,4},{1,5},{2,6},{3,7},{4,8},{5,9},{6,10},{7,11},{8,12},{9,13},{1... | collective-permute-start | bytes 1622024 | tf_op jit(solution)/shard_map/ppermute | solution.py:352
  76.1 0.8 copy-start.3
  76.1 1.0 %copy-start.4 = (bf16[264,1024]{1,0:T(8,128)(2,1)}, bf16[264,1024]{1,0:T(8,128)(2,1)S(1)}, u32[]{:S(2)}) copy-start(bf16[264,1024]{1,0:T(8,128)(2,1)S(1)} %collective-permute-done.10) | copy-start | bytes 1622020
where the time goes:
time: 94.5 us; the launch traced here: 94 us
  Pallas kernels  52.8 us (56%)
  starting transfers between devices  22.6 us (24%)
  waiting for transfers between devices  13.4 us (14%)
  local copies, waits for them, and re-layouts  3.52 us (4%)
    pallas_call x3, Pallas kernels, stage(): attend_stage(places, pieces, first, last)  48.5 us
    ppermute x12, starting transfers between devices, send(): return lax.ppermute(x, ('group', 'ctx'), toward(leading, step))  17.8 us
    ppermute x12, waiting for transfers between devices, send(): return lax.ppermute(x, ('group', 'ctx'), toward(leading, step))  13.4 us
    all_to_all x1, starting transfers between devices, whole_step(): lax.all_to_all(packed.reshape(8, 2, 2 * PAGE + 8, E), 'group', split_axis...  4.8 us
    pallas_call x1, Pallas kernels, pack_pages(): pl.pallas_call(kernel, in_specs=[pl.BlockSpec(memory_space=pltpu.SMEM), p...  2.34 us
    pallas_call x1, Pallas kernels, prepare(): pl.pallas_call(kernel, in_specs=[vmem] * 3, out_specs=[vmem] * 2, out_sha...  1.99 us
  transfers between devices with their start and end apart: 13, of which 4 were waited for; matrix products, arithmetic and copies ran while one was open for 3% of the time, Pallas kernels for 36%

commit v1 on v0

--- a/solution.py
+++ b/solution.py
@@ -62,15 +62,24 @@
         lane = lax.broadcasted_iota(jnp.int32, (T, T), 1)
         row = lax.broadcasted_iota(jnp.int32, (T, T), 0)
 
+        def copies(part):
+            at = 0
+            result = []
+            lanes = pl.ds(part * HK * E, HK * E)
+            for k, (ref, n) in enumerate(zip(operands, pieces)):
+                result.append(
+                    pltpu.make_async_copy(
+                        ref.at[:, :, lanes], kv.at[pl.ds(at, n), :, lanes], sems.at[part, k]
+                    )
+                )
+                at += n
+            return result
+
         def load():
-            copies = []
-            at = 0
-            for k, (ref, n) in enumerate(zip(operands, pieces)):
-                copy = pltpu.make_async_copy(ref, kv.at[pl.ds(at, n)], sems.at[k])
-                copy.start()
-                copies.append(copy)
-                at += n
-            for copy in copies:
+            for part in range(2):
+                for copy in copies(part):
+                    copy.start()
+            for copy in copies(0):
                 copy.wait()
             own = here_ref[0]
             swapped = here_ref[1] == 1
@@ -204,6 +213,11 @@
         def _():
             load()
             turn(True, False, 0)
+
+        @pl.when(step == 1)
+        def _():
+            for copy in copies(1):
+                copy.wait()
 
         @pl.when((step == 1) | (step == 3))
         def _():
@@ -262,7 +276,7 @@
             pltpu.VMEM((REP, E, T), jnp.float32),
             pltpu.VMEM((REP, 8, T), jnp.float32),
             pltpu.SMEM((32,), jnp.int32),
-            pltpu.SemaphoreType.DMA((len(pieces),)),
+            pltpu.SemaphoreType.DMA((2, len(pieces))),
         ],
         compiler_params=pltpu.CompilerParams(
             dimension_semantics=("arbitrary",), vmem_limit_bytes=58 * 1024 * 1024
@@ -356,15 +370,15 @@
 
     own, starts = prepare(keys, values, documents)
     up, down = send(own, True, 1), send(own, True, -1)
-    far = send(own, True, 2)
     own_up, own_down = send(own, False, 1), send(own, False, -1)
     packed = pack_pages(keys, values, owners[0, :, 0])
     arrived = lax.all_to_all(
         packed.reshape(8, 2, 2 * PAGE + 8, E), "group", split_axis=0, concat_axis=0, tiled=True
     ).reshape(16, 2 * PAGE + 8, E)
     up, down, packed = lax.optimization_barrier((up, down, packed))
+    far = send(up[:PAGE], True, 1), send(down[PAGE:], True, -1)
     up_up, up_down = send(up, False, 1), send(up, False, -1)
-    two = jnp.concatenate([down, far])
+    two = jnp.concatenate([down, *far])
     two_down, two_up = send(two, False, -1), send(two, False, 1)
     own_far = send(own_up, False, 1)
     up_far = send(up_up, False, 1)

time: 94.5 us -> 95.3 us (level)
  starting transfers between devices: 22.6 us -> 24.6 us
  Pallas kernels: 52.8 us -> 51.3 us
  waiting for transfers between devices: 13.4 us -> 14.6 us
    ppermute x12 -> x13, starting transfers between devices: 17.8 us -> 19.8 us  [send(): return lax.ppermute(x, ('group', 'ctx'), toward(leading, step))]
    pallas_call x3, Pallas kernels: 48.5 us -> 46.9 us  [stage(): attend_stage(places, pieces, first, last)]
    ppermute x12 -> x13, waiting for transfers between devices: 13.4 us -> 14.6 us  [send(): return lax.ppermute(x, ('group', 'ctx'), toward(leading, step))]
  transfers between devices with their start and end apart: 13 -> 14, of which waited for: 4 -> 4; matrix products, arithmetic and copies ran while one was open for 3% -> 2% of each run, Pallas kernels for 36% -> 35%
where the time goes in v1:
time: 95.3 us; the launch traced here: 94.7 us
  Pallas kernels  51.3 us (54%)
  starting transfers between devices  24.6 us (26%)
  waiting for transfers between devices  14.6 us (15%)
  local copies, waits for them, and re-layouts  2.77 us (3%)
    pallas_call x3, Pallas kernels, stage(): attend_stage(places, pieces, first, last)  46.9 us
    ppermute x13, starting transfers between devices, send(): return lax.ppermute(x, ('group', 'ctx'), toward(leading, step))  19.8 us
    ppermute x13, waiting for transfers between devices, send(): return lax.ppermute(x, ('group', 'ctx'), toward(leading, step))  14.6 us
    all_to_all x1, starting transfers between devices, whole_step(): lax.all_to_all(packed.reshape(8, 2, 2 * PAGE + 8, E), 'group', split_axis...  4.8 us
    pallas_call x1, Pallas kernels, pack_pages(): pl.pallas_call(kernel, in_specs=[pl.BlockSpec(memory_space=pltpu.SMEM), p...  2.33 us
    pallas_call x1, Pallas kernels, prepare(): pl.pallas_call(kernel, in_specs=[vmem] * 3, out_specs=[vmem] * 2, out_sha...  1.98 us
  transfers between devices with their start and end apart: 14, of which 4 were waited for; matrix products, arithmetic and copies ran while one was open for 2% of the time, Pallas kernels for 35%

profile of v1, /device:TPU:28, one launch (start us, length us, event | category | flops | bytes accessed | tf_op | source)
XLA Modules:
  0.0 94.7 jit_solution(8090582987975801725)
XLA Ops:
  0.6 2.0 %prepare.1 = (bf16[264,1024]{1,0:T(8,128)(2,1)}, s32[8,256]{1,0:T(8,128)}) custom-call(bf16[256,512]{1,0:T(8,128)(2,1)} %bitcast.27, bf16[256,512]{1,0:T(8,128)(2,1)} %bitcast.29, s32[1,256]{1,0:T(1,128)} %doc_ref.1), custom_call_target="tpu_custom_call" | custom-call | tf_op jit(solution)/shard_map/prepare/pallas_call | solution.py:348
  2.6 1.9 %collective-permute-start = (bf16[264,1024]{1,0:T(8,128)(2,1)}, bf16[264,1024]{1,0:T(8,128)(2,1)S(1)}, u32[]{:S(2)}, u32[]{:S(2)}) collective-permute-start(bf16[264,1024]{1,0:T(8,128)(2,1)} %get-tuple-element.14), channel_id=1, source_target_pairs={{0,1},{1,2},{2,3},{3,0},{4,5},{5,6},{6,7},{7,4},{8,9},{9,10},{10,1... | collective-permute-start | bytes 1622024 | tf_op jit(solution)/shard_map/ppermute | solution.py:366
  4.5 2.1 %collective-permute-start.1 = (bf16[264,1024]{1,0:T(8,128)(2,1)}, bf16[264,1024]{1,0:T(8,128)(2,1)S(1)}, u32[]{:S(2)}, u32[]{:S(2)}) collective-permute-start(bf16[264,1024]{1,0:T(8,128)(2,1)} %get-tuple-element.14), channel_id=1, source_target_pairs={{0,3},{1,0},{2,1},{3,2},{4,7},{5,4},{6,5},{7,6},{8,11},{9,8},{10,9... | collective-permute-start | bytes 1622024 | tf_op jit(solution)/shard_map/ppermute | solution.py:366
  6.7 2.3 %pack_pages.1 = bf16[16,264,128]{2,1,0:T(8,128)(2,1)} custom-call(s32[8]{0:T(128)} %bitcast.36, bf16[256,512]{1,0:T(8,128)(2,1)} %bitcast.28, bf16[256,512]{1,0:T(8,128)(2,1)} %bitcast.30), custom_call_target="tpu_custom_call" | custom-call | tf_op jit(solution)/shard_map/pack_pages/pallas_call | solution.py:315
  9.0 5.2 %collective-permute-done = bf16[264,1024]{1,0:T(8,128)(2,1)S(1)} collective-permute-done((bf16[264,1024]{1,0:T(8,128)(2,1)}, bf16[264,1024]{1,0:T(8,128)(2,1)S(1)}, u32[]{:S(2)}, u32[]{:S(2)}) %collective-permute-start) | collective-permute-done | bytes 540704 | tf_op jit(solution)/shard_map/ppermute | solution.py:366
  14.2 0.0 copy-start.1
  14.2 0.0 collective-permute-done.1
  14.2 1.9 %collective-permute-start.2 = (bf16[128,1024]{1,0:T(8,128)(2,1)S(1)}, bf16[128,1024]{1,0:T(8,128)(2,1)S(1)}, u32[]{:S(2)}, u32[]{:S(2)}) collective-permute-start(bf16[128,1024]{1,0:T(8,128)(2,1)S(1)} %slice.12), channel_id=1, source_target_pairs={{0,1},{1,2},{2,3},{3,0},{4,5},{5,6},{6,7},{7,4},{8,9},{9,10},{10,1... | collective-permute-start | bytes 786440 | tf_op jit(solution)/shard_map/ppermute | solution.py:366
  16.1 0.0 copy-start.2
  16.1 1.5 %collective-permute-start.3 = (bf16[136,1024]{1,0:T(8,128)(2,1)S(1)}, bf16[136,1024]{1,0:T(8,128)(2,1)S(1)}, u32[]{:S(2)}, u32[]{:S(2)}) collective-permute-start(bf16[136,1024]{1,0:T(8,128)(2,1)S(1)} %slice.13), channel_id=1, source_target_pairs={{0,3},{1,0},{2,1},{3,2},{4,7},{5,4},{6,5},{7,6},{8,11},{9,8},{10,9... | collective-permute-start | bytes 835592 | tf_op jit(solution)/shard_map/ppermute | solution.py:366
  17.7 4.2 %collective-permute-done.2 = bf16[128,1024]{1,0:T(8,128)(2,1)S(1)} collective-permute-done((bf16[128,1024]{1,0:T(8,128)(2,1)S(1)}, bf16[128,1024]{1,0:T(8,128)(2,1)S(1)}, u32[]{:S(2)}, u32[]{:S(2)}) %collective-permute-start.2) | collective-permute-done | bytes 262176 | tf_op jit(solution)/shard_map/ppermute | solution.py:366
  21.9 1.4 %collective-permute-done.3 = bf16[136,1024]{1,0:T(8,128)(2,1)S(1)} collective-permute-done((bf16[136,1024]{1,0:T(8,128)(2,1)S(1)}, bf16[136,1024]{1,0:T(8,128)(2,1)S(1)}, u32[]{:S(2)}, u32[]{:S(2)}) %collective-permute-start.3) | collective-permute-done | bytes 278560 | tf_op jit(solution)/shard_map/ppermute | solution.py:366
  23.3 0.0 copy-start
  23.4 1.0 %collective-permute-start.9 = (bf16[528,1024]{1,0:T(8,128)(2,1)S(1)}, bf16[528,1024]{1,0:T(8,128)(2,1)}, u32[]{:S(2)}, u32[]{:S(2)}) collective-permute-start(bf16[528,1024]{1,0:T(8,128)(2,1)S(1)} %constant_dynamic-update-slice_fusion), channel_id=1, source_target_pairs={{0,12},{1,13},{2,14},{3,15},{4,0},{5,1},{6,2},{7,3},{8,4},{9,5},{1... | collective-permute-start | bytes 3244040 | tf_op jit(solution)/shard_map/ppermute | solution.py:366
  24.4 0.0 copy-done.2
  24.4 2.3 %collective-permute-start.4 = (bf16[264,1024]{1,0:T(8,128)(2,1)S(1)}, bf16[264,1024]{1,0:T(8,128)(2,1)}, u32[]{:S(2)}, u32[]{:S(2)}) collective-permute-start(bf16[264,1024]{1,0:T(8,128)(2,1)S(1)} %copy-done.2), channel_id=1, source_target_pairs={{0,4},{1,5},{2,6},{3,7},{4,8},{5,9},{6,10},{7,11},{8,12},{9,13},{1... | collective-permute-start | bytes 1622024 | tf_op jit(solution)/shard_map/ppermute | solution.py:366
  26.7 0.0 collective-permute-start.6
  26.7 0.0 copy-done
  26.7 4.8 %all-to-all-start = ((bf16[8,2,264,128]{3,2,1,0:T(8,128)(2,1)}), bf16[8,2,264,128]{3,2,1,0:T(8,128)(2,1)S(1)}, u32[]{:S(2)}, u32[]{:S(2)}) async-start(bf16[8,2,264,128]{3,2,1,0:T(8,128)(2,1)} %bitcast.20), calls=%async_computation | async-start | bytes 2162688 | tf_op jit(solution)/shard_map/all_to_all | solution.py:375
  31.5 2.0 %collective-permute-start.7 = (bf16[264,1024]{1,0:T(8,128)(2,1)S(1)}, bf16[264,1024]{1,0:T(8,128)(2,1)}, u32[]{:S(2)}, u32[]{:S(2)}) collective-permute-start(bf16[264,1024]{1,0:T(8,128)(2,1)S(1)} %copy-done.2), channel_id=1, source_target_pairs={{0,12},{1,13},{2,14},{3,15},{4,0},{5,1},{6,2},{7,3},{8,4},{9,5},{1... | collective-permute-start | bytes 1622024 | tf_op jit(solution)/shard_map/ppermute | solution.py:366
  33.5 1.2 %collective-permute-start.5 = (bf16[264,1024]{1,0:T(8,128)(2,1)S(1)}, bf16[264,1024]{1,0:T(8,128)(2,1)}, u32[]{:S(2)}, u32[]{:S(2)}) collective-permute-start(bf16[264,1024]{1,0:T(8,128)(2,1)S(1)} %collective-permute-done), channel_id=1, source_target_pairs={{0,4},{1,5},{2,6},{3,7},{4,8},{5,9},{6,10},{7,11},{8,12},{9,13},{1... | collective-permute-start | bytes 1622024 | tf_op jit(solution)/shard_map/ppermute | solution.py:366
  34.7 0.0 collective-permute-done.4
  34.7 0.0 copy-done.1
  34.7 0.8 collective-permute-start.8
  35.5 0.6 pad_add_fusion.refs_0_
  36.1 3.7 %collective-permute-done.9 = bf16[528,1024]{1,0:T(8,128)(2,1)} collective-permute-done((bf16[528,1024]{1,0:T(8,128)(2,1)S(1)}, bf16[528,1024]{1,0:T(8,128)(2,1)}, u32[]{:S(2)}, u32[]{:S(2)}) %collective-permute-start.9) | collective-permute-done | bytes 1081376 | tf_op jit(solution)/shard_map/ppermute | solution.py:366
  39.9 0.0 collective-permute-start.12
  39.9 8.2 %attend_first.1 = (f32[32,128,256]{2,1,0:T(8,128)}, f32[32,8,256]{2,1,0:T(8,128)}, f32[32,8,256]{2,1,0:T(8,128)}) custom-call(s32[2]{0:T(128)} %pad_add_fusion.refs_0_, s32[256]{0:T(256)} %bitcast.33, s32[8,256]{1,0:T(8,128)} %get-tuple-element.13.refs_2_, bf16[256,4096]{1,0:T(8,128)(2,1)} %bitcast.38, bf16[1,264,1024]{2,1,0:T(8,128)(2,1)} %bitcast.41, ...), custom_call_target="tpu_custom_call" | custom-call | flops 4294967296 | bytes 4194304 | tf_op jit(solution)/shard_map/attend_first/pallas_call | solution.py:393
  48.1 0.0 all-to-all-done
  48.1 1.1 %slice.16 = bf16[16,256,128]{2,1,0:T(8,128)(2,1)} slice(bf16[16,264,128]{2,1,0:T(8,128)(2,1)S(1)} %bitcast.24), slice={[0:16], [0:256], [0:128]} | slice | bytes 2097152 | tf_op jit(solution)/shard_map/slice | solution.py:401
  49.1 0.6 copy.10
  49.7 0.0 collective-permute-done.7
  49.7 3.2 %collective-permute-start.10 = (bf16[264,1024]{1,0:T(8,128)(2,1)}, bf16[264,1024]{1,0:T(8,128)(2,1)S(1)}, u32[]{:S(2)}, u32[]{:S(2)}) collective-permute-start(bf16[264,1024]{1,0:T(8,128)(2,1)} %collective-permute-done.4), channel_id=1, source_target_pairs={{0,4},{1,5},{2,6},{3,7},{4,8},{5,9},{6,10},{7,11},{8,12},{9,13},{1... | collective-permute-start | bytes 1622024 | tf_op jit(solution)/shard_map/ppermute | solution.py:366
  53.0 0.0 collective-permute-done.5
  53.0 1.7 %collective-permute-start.11 = (bf16[264,1024]{1,0:T(8,128)(2,1)}, bf16[264,1024]{1,0:T(8,128)(2,1)S(1)}, u32[]{:S(2)}, u32[]{:S(2)}) collective-permute-start(bf16[264,1024]{1,0:T(8,128)(2,1)} %collective-permute-done.5), channel_id=1, source_target_pairs={{0,4},{1,5},{2,6},{3,7},{4,8},{5,9},{6,10},{7,11},{8,12},{9,13},{1... | collective-permute-start | bytes 1622024 | tf_op jit(solution)/shard_map/ppermute | solution.py:366
  54.7 0.0 collective-permute-done.8
  54.7 0.0 collective-permute-done.6
  54.7 22.4 %attend_middle.1 = (f32[32,128,256]{2,1,0:T(8,128)}, f32[32,8,256]{2,1,0:T(8,128)}, f32[32,8,256]{2,1,0:T(8,128)}) custom-call(s32[2]{0:T(128)} %pad_add_fusion.refs_0_, s32[256]{0:T(256)} %bitcast.34, s32[8,256]{1,0:T(8,128)} %get-tuple-element.13.refs_2_, bf16[256,4096]{1,0:T(8,128)(2,1)} %bitcast.39, f32[32,128,256]{2,1,0:T(8,128)} %get-tuple-element.17.refs_4_, ...), custom_call_target="tpu_custom_call" | custom-call | flops 8589934592 | bytes 4194304 | tf_op jit(solution)/shard_map/attend_middle/pallas_call | solution.py:393
  77.1 0.0 collective-permute-done.10
  77.2 0.0 copy-start.3
  77.2 0.0 collective-permute-done.11
  77.2 0.0 copy-start.4
  77.2 0.0 collective-permute-done.12
  77.2 0.8 copy-done.3
  78.0 0.2 copy-done.4
  78.2 16.4 %attend_last.1 = bf16[256,4096]{1,0:T(8,128)(2,1)} custom-call(s32[2]{0:T(128)} %pad_add_fusion.refs_0_, s32[256]{0:T(256)} %bitcast.35, s32[8,256]{1,0:T(8,128)} %get-tuple-element.13.refs_2_, bf16[256,4096]{1,0:T(8,128)(2,1)} %bitcast.40, f32[32,128,256]{2,1,0:T(8,128)} %get-tuple-element.20.refs_4_, f32[32,8,256]{2,1,0:T(8,128)} %get-tuple-element.21.refs_5_, ...), custom_call_target="tpu_custom_call" | custom-call | flops 4294967296 | bytes 4194304 | tf_op jit(solution)/shard_map/attend_last/pallas_call | solution.py:393
  (6 shorter events, 0.1 us)
Async XLA Ops:
  2.6 11.6 %collective-permute-start = (bf16[264,1024]{1,0:T(8,128)(2,1)}, bf16[264,1024]{1,0:T(8,128)(2,1)S(1)}, u32[]{:S(2)}, u32[]{:S(2)}) collective-permute-start(bf16[264,1024]{1,0:T(8,128)(2,1)} %get-tuple-element.14), channel_id=1, source_target_pairs={{0,1},{1,2},{2,3},{3,0},{4,5},{5,6},{6,7},{7,4},{8,9},{9,10},{10,1... | collective-permute-start | bytes 1622024 | tf_op jit(solution)/shard_map/ppermute | solution.py:366
  4.5 9.7 %collective-permute-start.1 = (bf16[264,1024]{1,0:T(8,128)(2,1)}, bf16[264,1024]{1,0:T(8,128)(2,1)S(1)}, u32[]{:S(2)}, u32[]{:S(2)}) collective-permute-start(bf16[264,1024]{1,0:T(8,128)(2,1)} %get-tuple-element.14), channel_id=1, source_target_pairs={{0,3},{1,0},{2,1},{3,2},{4,7},{5,4},{6,5},{7,6},{8,11},{9,8},{10,9... | collective-permute-start | bytes 1622024 | tf_op jit(solution)/shard_map/ppermute | solution.py:366
  14.2 20.5 %copy-start.1 = (bf16[264,1024]{1,0:T(8,128)(2,1)}, bf16[264,1024]{1,0:T(8,128)(2,1)S(1)}, u32[]{:S(2)}) copy-start(bf16[264,1024]{1,0:T(8,128)(2,1)S(1)} %collective-permute-done) | copy-start | bytes 1622020
  14.2 7.7 %collective-permute-start.2 = (bf16[128,1024]{1,0:T(8,128)(2,1)S(1)}, bf16[128,1024]{1,0:T(8,128)(2,1)S(1)}, u32[]{:S(2)}, u32[]{:S(2)}) collective-permute-start(bf16[128,1024]{1,0:T(8,128)(2,1)S(1)} %slice.12), channel_id=1, source_target_pairs={{0,1},{1,2},{2,3},{3,0},{4,5},{5,6},{6,7},{7,4},{8,9},{9,10},{10,1... | collective-permute-start | bytes 786440 | tf_op jit(solution)/shard_map/ppermute | solution.py:366
  16.1 8.3 %copy-start.2 = (bf16[264,1024]{1,0:T(8,128)(2,1)S(1)}, bf16[264,1024]{1,0:T(8,128)(2,1)}, u32[]{:S(2)}) copy-start(bf16[264,1024]{1,0:T(8,128)(2,1)} %get-tuple-element.14) | copy-start | bytes 1622020
  16.1 7.2 %collective-permute-start.3 = (bf16[136,1024]{1,0:T(8,128)(2,1)S(1)}, bf16[136,1024]{1,0:T(8,128)(2,1)S(1)}, u32[]{:S(2)}, u32[]{:S(2)}) collective-permute-start(bf16[136,1024]{1,0:T(8,128)(2,1)S(1)} %slice.13), channel_id=1, source_target_pairs={{0,3},{1,0},{2,1},{3,2},{4,7},{5,4},{6,5},{7,6},{8,11},{9,8},{10,9... | collective-permute-start | bytes 835592 | tf_op jit(solution)/shard_map/ppermute | solution.py:366
  23.3 3.3 %copy-start = (bf16[528,1024]{1,0:T(8,128)(2,1)}, bf16[528,1024]{1,0:T(8,128)(2,1)S(1)}, u32[]{:S(2)}) copy-start(bf16[528,1024]{1,0:T(8,128)(2,1)S(1)} %constant_dynamic-update-slice_fusion) | copy-start | bytes 3244036
  23.4 16.5 %collective-permute-start.9 = (bf16[528,1024]{1,0:T(8,128)(2,1)S(1)}, bf16[528,1024]{1,0:T(8,128)(2,1)}, u32[]{:S(2)}, u32[]{:S(2)}) collective-permute-start(bf16[528,1024]{1,0:T(8,128)(2,1)S(1)} %constant_dynamic-update-slice_fusion), channel_id=1, source_target_pairs={{0,12},{1,13},{2,14},{3,15},{4,0},{5,1},{6,2},{7,3},{8,4},{9,5},{1... | collective-permute-start | bytes 3244040 | tf_op jit(solution)/shard_map/ppermute | solution.py:366
  24.4 10.3 %collective-permute-start.4 = (bf16[264,1024]{1,0:T(8,128)(2,1)S(1)}, bf16[264,1024]{1,0:T(8,128)(2,1)}, u32[]{:S(2)}, u32[]{:S(2)}) collective-permute-start(bf16[264,1024]{1,0:T(8,128)(2,1)S(1)} %copy-done.2), channel_id=1, source_target_pairs={{0,4},{1,5},{2,6},{3,7},{4,8},{5,9},{6,10},{7,11},{8,12},{9,13},{1... | collective-permute-start | bytes 1622024 | tf_op jit(solution)/shard_map/ppermute | solution.py:366
  26.7 28.1 %collective-permute-start.6 = (bf16[528,1024]{1,0:T(8,128)(2,1)S(1)}, bf16[528,1024]{1,0:T(8,128)(2,1)}, u32[]{:S(2)}, u32[]{:S(2)}) collective-permute-start(bf16[528,1024]{1,0:T(8,128)(2,1)S(1)} %constant_dynamic-update-slice_fusion), channel_id=1, source_target_pairs={{0,4},{1,5},{2,6},{3,7},{4,8},{5,9},{6,10},{7,11},{8,12},{9,13},{1... | collective-permute-start | bytes 3244040 | tf_op jit(solution)/shard_map/ppermute | solution.py:366
  26.7 21.4 %all-to-all-start = ((bf16[8,2,264,128]{3,2,1,0:T(8,128)(2,1)}), bf16[8,2,264,128]{3,2,1,0:T(8,128)(2,1)S(1)}, u32[]{:S(2)}, u32[]{:S(2)}) async-start(bf16[8,2,264,128]{3,2,1,0:T(8,128)(2,1)} %bitcast.20), calls=%async_computation | async-start | bytes 2162688 | tf_op jit(solution)/shard_map/all_to_all | solution.py:375
  31.5 18.3 %collective-permute-start.7 = (bf16[264,1024]{1,0:T(8,128)(2,1)S(1)}, bf16[264,1024]{1,0:T(8,128)(2,1)}, u32[]{:S(2)}, u32[]{:S(2)}) collective-permute-start(bf16[264,1024]{1,0:T(8,128)(2,1)S(1)} %copy-done.2), channel_id=1, source_target_pairs={{0,12},{1,13},{2,14},{3,15},{4,0},{5,1},{6,2},{7,3},{8,4},{9,5},{1... | collective-permute-start | bytes 1622024 | tf_op jit(solution)/shard_map/ppermute | solution.py:366
  33.5 19.5 %collective-permute-start.5 = (bf16[264,1024]{1,0:T(8,128)(2,1)S(1)}, bf16[264,1024]{1,0:T(8,128)(2,1)}, u32[]{:S(2)}, u32[]{:S(2)}) collective-permute-start(bf16[264,1024]{1,0:T(8,128)(2,1)S(1)} %collective-permute-done), channel_id=1, source_target_pairs={{0,4},{1,5},{2,6},{3,7},{4,8},{5,9},{6,10},{7,11},{8,12},{9,13},{1... | collective-permute-start | bytes 1622024 | tf_op jit(solution)/shard_map/ppermute | solution.py:366
  34.7 20.0 %collective-permute-start.8 = (bf16[264,1024]{1,0:T(8,128)(2,1)S(1)}, bf16[264,1024]{1,0:T(8,128)(2,1)}, u32[]{:S(2)}, u32[]{:S(2)}) collective-permute-start(bf16[264,1024]{1,0:T(8,128)(2,1)S(1)} %collective-permute-done), channel_id=1, source_target_pairs={{0,12},{1,13},{2,14},{3,15},{4,0},{5,1},{6,2},{7,3},{8,4},{9,5},{1... | collective-permute-start | bytes 1622024 | tf_op jit(solution)/shard_map/ppermute | solution.py:366
  39.9 37.3 %collective-permute-start.12 = (bf16[528,1024]{1,0:T(8,128)(2,1)}, bf16[528,1024]{1,0:T(8,128)(2,1)}, u32[]{:S(2)}, u32[]{:S(2)}) collective-permute-start(bf16[528,1024]{1,0:T(8,128)(2,1)} %collective-permute-done.9), channel_id=1, source_target_pairs={{0,12},{1,13},{2,14},{3,15},{4,0},{5,1},{6,2},{7,3},{8,4},{9,5},{1... | collective-permute-start | bytes 3244040 | tf_op jit(solution)/shard_map/ppermute | solution.py:366
  49.7 27.4 %collective-permute-start.10 = (bf16[264,1024]{1,0:T(8,128)(2,1)}, bf16[264,1024]{1,0:T(8,128)(2,1)S(1)}, u32[]{:S(2)}, u32[]{:S(2)}) collective-permute-start(bf16[264,1024]{1,0:T(8,128)(2,1)} %collective-permute-done.4), channel_id=1, source_target_pairs={{0,4},{1,5},{2,6},{3,7},{4,8},{5,9},{6,10},{7,11},{8,12},{9,13},{1... | collective-permute-start | bytes 1622024 | tf_op jit(solution)/shard_map/ppermute | solution.py:366
  53.0 24.2 %collective-permute-start.11 = (bf16[264,1024]{1,0:T(8,128)(2,1)}, bf16[264,1024]{1,0:T(8,128)(2,1)S(1)}, u32[]{:S(2)}, u32[]{:S(2)}) collective-permute-start(bf16[264,1024]{1,0:T(8,128)(2,1)} %collective-permute-done.5), channel_id=1, source_target_pairs={{0,4},{1,5},{2,6},{3,7},{4,8},{5,9},{6,10},{7,11},{8,12},{9,13},{1... | collective-permute-start | bytes 1622024 | tf_op jit(solution)/shard_map/ppermute | solution.py:366
  77.2 0.8 copy-start.3
  77.2 1.0 %copy-start.4 = (bf16[264,1024]{1,0:T(8,128)(2,1)}, bf16[264,1024]{1,0:T(8,128)(2,1)S(1)}, u32[]{:S(2)}) copy-start(bf16[264,1024]{1,0:T(8,128)(2,1)S(1)} %collective-permute-done.11) | copy-start | bytes 1622020
